TPU v7x, 32 devices: a whole 2x2x4 slice. The times are simulated.
32 devices in a mesh: dp: 4 (over x, core), fsdp: 8 (over z, y).
Axes of the slice: x: 2, y: 2, z: 4, core: 2. Of those that a mesh axis runs over, the one named last changes fastest.
Arguments:
- frames: bfloat16 [8, 1024, 1024], P('fsdp', 'dp'), may hold values from -6 to 6
- cotangent: bfloat16 [8, 1024, 1024], P('fsdp', 'dp'), may hold values from -6 to 6
- phon_len: int32 [8], replicated, may hold values from 32 to 128
- acou_len: int32 [8], replicated, may hold values from 128 to 895
- row_item: int32 [8], P('fsdp'), may hold values from 0 to 7, each once
- w_qkv: bfloat16 [1024, 3072], P(('dp', 'fsdp')), may hold values from -0.1875 to 0.1875
- w_out: bfloat16 [1024, 1024], P(('dp', 'fsdp')), may hold values from -2 to 2
- w_up: bfloat16 [1024, 4096], P(('dp', 'fsdp')), may hold values from -0.1875 to 0.1875
- w_down: bfloat16 [4096, 1024], P(('dp', 'fsdp')), may hold values from -0.09375 to 0.09375
- ln1_gain: bfloat16 [1024], P(('dp', 'fsdp')), may hold values from 0.25 to 1.75
- ln1_bias: bfloat16 [1024], P(('dp', 'fsdp')), may hold values from -2.5 to 2.5
- ln2_gain: bfloat16 [1024], P(('dp', 'fsdp')), may hold values from 0.25 to 1.75
- ln2_bias: bfloat16 [1024], P(('dp', 'fsdp')), may hold values from -2.5 to 2.5
Outputs:
- activations: bfloat16 [8, 1024, 1024], P('fsdp', 'dp')
- input_grad: float32 [8, 1024, 1024], P('fsdp', 'dp')
- w_qkv_grad: float32 [1024, 3072], P(('dp', 'fsdp'))
- w_out_grad: float32 [1024, 1024], P(('dp', 'fsdp'))
- w_up_grad: float32 [1024, 4096], P(('dp', 'fsdp'))
- w_down_grad: float32 [4096, 1024], P(('dp', 'fsdp'))
- ln1_gain_grad: float32 [1024], P(('dp', 'fsdp'))
- ln1_bias_grad: float32 [1024], P(('dp', 'fsdp'))
- ln2_gain_grad: float32 [1024], P(('dp', 'fsdp'))
- ln2_bias_grad: float32 [1024], P(('dp', 'fsdp'))
Inputs may be any that keep to these rules, and one draw needn't show every extreme that they name: `acou_len`: an item's phoneme and acoustic lengths together are under 1024. `row_item`: each row holds a different item.
All inputs are finite; a program needn't handle non-finite values.
Results may differ from a plain program's by a relative error of at most 0.011.
Values may be sent and summed in bfloat16 or wider, within the bound.
A program may use at most 256 MiB of HBM per device.

v0:
```python
import functools

import jax
import jax.numpy as jnp
from jax import lax
from jax.experimental import pallas as pl
from jax.experimental.pallas import tpu as pltpu
from jax.sharding import PartitionSpec as P

HEAD_DIM = 64
EPS = 1e-05
MASKED = -1e30
BLOCK = 256

f32 = jnp.float32
bf16 = jnp.bfloat16


def dot(a, b, ca, cb):
    return lax.dot_general(a, b, (((ca,), (cb,)), ((), ())), preferred_element_type=f32)


def row_limit(start, rows, phon, acou):
    pos = start + lax.broadcasted_iota(jnp.int32, (1, rows), 1)
    return jnp.where(pos < phon + acou, jnp.maximum(pos, phon - 1), phon - 1)


def head_mask(width, head):
    lane = lax.broadcasted_iota(jnp.int32, (1, width), 1)
    return (lane >= head * HEAD_DIM) & (lane < (head + 1) * HEAD_DIM)


def attn_fwd_kernel(lens, qkv, out, lse, between={}):
    width = out.shape[1]
    heads = width // HEAD_DIM
    length = out.shape[0]
    phon, acou = lens[0], lens[1]
    scale = HEAD_DIM ** (-0.5)
    for start in range(0, length, BLOCK):
        if start // BLOCK in between:
            between[start // BLOCK]()
        seen = start + BLOCK
        q = qkv[start : start + BLOCK, :width] * scale
        k = qkv[:seen, width : 2 * width]
        v = qkv[:seen, 2 * width :]
        limit = row_limit(start, BLOCK, phon, acou)
        key = lax.broadcasted_iota(jnp.int32, (seen, 1), 0)
        hidden = key > limit
        total = jnp.zeros((BLOCK, width), f32)
        rows = []
        for h in range(heads):
            mine = head_mask(width, h)
            qh = jnp.where(mine, q, 0)
            s = dot(k, qh, 1, 1)
            s = jnp.where(hidden, MASKED, s)
            top = jnp.max(s, axis=0, keepdims=True)
            e = jnp.exp(s - top)
            tot = jnp.sum(e, axis=0, keepdims=True)
            p = (e * (1.0 / tot)).astype(bf16)
            o = dot(p, v, 0, 0)
            total = total + jnp.where(mine, o, 0)
            rows.append(top + jnp.log(tot))
        out[start : start + BLOCK, :] = total.astype(bf16)
        lse[:, start : start + BLOCK] = jnp.concatenate(rows + [jnp.zeros((8 - heads, BLOCK), f32)], axis=0)


def attn_bwd_kernel(lens, qkv, grad, lse, dqkv, dk_acc, dv_acc, between={}):
    width = grad.shape[2]
    heads = width // HEAD_DIM
    length = grad.shape[0] * BLOCK
    phon, acou = lens[0], lens[1]
    scale = HEAD_DIM ** (-0.5)
    dk_acc[...] = jnp.zeros_like(dk_acc)
    dv_acc[...] = jnp.zeros_like(dv_acc)
    for start in reversed(range(0, length, BLOCK)):
        if start // BLOCK in between:
            between[start // BLOCK]()
        seen = start + BLOCK
        limit = row_limit(start, BLOCK, phon, acou)

        def two_heads(two, dq):
            q = qkv[start : start + BLOCK, :width] * scale
            g = grad[start // BLOCK]
            k = qkv[:seen, width : 2 * width]
            v = qkv[:seen, 2 * width :]
            hidden = lax.broadcasted_iota(jnp.int32, (seen, 1), 0) > limit
            for h in (2 * two, 2 * two + 1):
                mine = head_mask(width, h)
                qh = jnp.where(mine, q, 0)
                gh = jnp.where(mine, g, 0)
                s = dot(k, qh, 1, 1)
                s = jnp.where(hidden, MASKED, s)
                p = jnp.exp(s - lse[pl.ds(h, 1), start : start + BLOCK])
                gp = dot(v, gh, 1, 1)
                delta = jnp.sum(p * gp, axis=0, keepdims=True)
                ds = (p * (gp - delta)).astype(bf16)
                dvh = dot(p.astype(bf16), gh, 1, 0)
                dkh = dot(ds, qh, 1, 0)
                dv_acc[: seen // BLOCK] += dvh.reshape(seen // BLOCK, BLOCK, width)
                dk_acc[: seen // BLOCK] += dkh.reshape(seen // BLOCK, BLOCK, width)
                dq = dq + jnp.where(mine, dot(ds, k, 0, 0), 0)
            return dq

        dq = lax.fori_loop(0, heads // 2, two_heads, jnp.zeros((BLOCK, width), f32))
        dqkv[start // BLOCK, :, :width] = (dq * scale).astype(bf16)
    dqkv[:, :, width : 2 * width] = dk_acc[...].astype(bf16)
    dqkv[:, :, 2 * width :] = dv_acc[...].astype(bf16)


VMEM = pl.BlockSpec(memory_space=pltpu.VMEM)
SMEM = pl.BlockSpec(memory_space=pltpu.SMEM)


def attn_fwd(lens, qkv):
    length, width = qkv.shape[0], qkv.shape[1] // 3
    return pl.pallas_call(
        attn_fwd_kernel,
        out_shape=(jax.ShapeDtypeStruct((length, width), bf16), jax.ShapeDtypeStruct((8, length), f32)),
        in_specs=[SMEM, VMEM],
        out_specs=(VMEM, VMEM),
        compiler_params=pltpu.CompilerParams(vmem_limit_bytes=40 * 2**20),
        cost_estimate=pl.CostEstimate(flops=4 * length * length * width, bytes_accessed=8 * length * width, transcendentals=length * length * width // HEAD_DIM),
        name="attn_fwd",
    )(lens, qkv)


def attn_bwd(lens, qkv, grad, lse):
    length, width = grad.shape
    blocks = length // BLOCK
    out = pl.pallas_call(
        attn_bwd_kernel,
        out_shape=jax.ShapeDtypeStruct((blocks, BLOCK, 3 * width), bf16),
        in_specs=[SMEM, VMEM, VMEM, VMEM],
        out_specs=VMEM,
        scratch_shapes=[pltpu.VMEM((blocks, BLOCK, width), f32)] * 2,
        compiler_params=pltpu.CompilerParams(vmem_limit_bytes=40 * 2**20),
        cost_estimate=pl.CostEstimate(flops=10 * length * length * width, bytes_accessed=14 * length * width, transcendentals=length * length * width // HEAD_DIM),
        name="attn_bwd",
    )(lens, qkv, grad.reshape(blocks, BLOCK, width), lse)
    return out.reshape(length, 3 * width)


def norm_parts(v):
    mean = jnp.mean(v, axis=-1, keepdims=True)
    centered = v - mean
    var = jnp.mean(centered * centered, axis=-1, keepdims=True)
    inv = lax.rsqrt(var + EPS)
    return centered * inv, inv


def norm_back(n, inv, gain, grad):
    g = grad * gain
    dx = inv * (g - jnp.mean(g, axis=-1, keepdims=True) - n * jnp.mean(g * n, axis=-1, keepdims=True))
    return dx, jnp.sum(grad * n, axis=0), jnp.sum(grad, axis=0)


def with_collectives(frames, cotangent, phon_len, acou_len, row_item, w_qkv, w_out, w_up, w_down, ln1_gain, ln1_bias, ln2_gain, ln2_bias):
    tp, dpn, fsn = "dp", lax.axis_size("dp"), lax.axis_size("fsdp")
    width = frames.shape[2]
    part = width // dpn
    rows = w_up.shape[0]

    vecs = jnp.concatenate([ln1_gain, ln1_bias, ln2_gain, ln2_bias])[None]
    vecs = lax.all_gather(vecs, ("dp", "fsdp"), axis=0, tiled=True)
    vecs = vecs.reshape(dpn * fsn, 4, rows).transpose(1, 0, 2).reshape(4, width).astype(f32)

    qkv_cols = w_qkv.reshape(rows, 3, dpn, part).transpose(2, 0, 1, 3).reshape(dpn, rows, 3 * part)
    qkv_cols = lax.all_to_all(qkv_cols, tp, 0, 0, tiled=True)
    wq = lax.all_gather(qkv_cols, "fsdp", axis=1, tiled=True).reshape(width, 3 * part)
    wo = lax.all_gather(w_out, "fsdp", axis=0, tiled=True)
    ff = w_up.shape[1] // dpn
    up_cols = w_up.reshape(rows, dpn, ff).transpose(1, 0, 2)
    up_cols = lax.all_to_all(up_cols, tp, 0, 0, tiled=True)
    wu = lax.all_gather(up_cols, "fsdp", axis=1, tiled=True).reshape(width, ff)
    wd = lax.all_gather(w_down, "fsdp", axis=0, tiled=True)

    item = row_item[0]
    pick = jnp.arange(phon_len.shape[0], dtype=jnp.int32) == item
    lens = jnp.stack([jnp.sum(jnp.where(pick, phon_len, 0)), jnp.sum(jnp.where(pick, acou_len, 0))])

    x = frames[0].astype(f32)
    n1, inv1 = norm_parts(x)
    normed1 = lax.all_gather((n1 * vecs[0] + vecs[1]).astype(bf16), tp, axis=0, tiled=True)
    grad_down = lax.all_gather(cotangent[0], tp, axis=0, tiled=True)
    qkv = jnp.dot(normed1, wq, preferred_element_type=f32).astype(bf16)
    attn_out, lse = attn_fwd(lens, qkv)
    proj = jnp.dot(attn_out, wo, preferred_element_type=f32).astype(bf16)
    middle = x + lax.psum_scatter(proj, tp, scatter_dimension=0, tiled=True).astype(f32)
    n2, inv2 = norm_parts(middle)
    normed2 = lax.all_gather((n2 * vecs[2] + vecs[3]).astype(bf16), tp, axis=0, tiled=True)
    up_out = jnp.dot(normed2, wu, preferred_element_type=f32)
    cdf = 0.5 * (1.0 + lax.erf(up_out * (0.5**0.5)))
    act_out = (up_out * cdf).astype(bf16)
    down = jnp.dot(act_out, wd, preferred_element_type=f32).astype(bf16)
    result = (middle + lax.psum_scatter(down, tp, scatter_dimension=0, tiled=True).astype(f32)).astype(bf16)

    g_down = dot(act_out, grad_down, 0, 0).astype(bf16)
    slope = cdf + up_out * (jnp.exp(-0.5 * up_out * up_out) * (1.0 / (2.0 * jnp.pi) ** 0.5))
    grad_up = (dot(grad_down, wd, 1, 1) * slope).astype(bf16)
    g_up = dot(normed2, grad_up, 0, 0).astype(bf16)
    grad_norm2 = lax.psum_scatter(dot(grad_up, wu, 1, 1).astype(bf16), tp, scatter_dimension=0, tiled=True).astype(f32)
    mid_norm, g_gain2, g_bias2 = norm_back(n2, inv2, vecs[2], grad_norm2)
    grad_middle = cotangent[0].astype(f32) + mid_norm
    grad_proj = lax.all_gather(grad_middle.astype(bf16), tp, axis=0, tiled=True)
    g_out = dot(attn_out, grad_proj, 0, 0).astype(bf16)
    grad_attn = dot(grad_proj, wo, 1, 1).astype(bf16)
    grad_qkv = attn_bwd(lens, qkv, grad_attn, lse)
    g_qkv = dot(normed1, grad_qkv, 0, 0).astype(bf16)
    grad_norm1 = lax.psum_scatter(dot(grad_qkv, wq, 1, 1).astype(bf16), tp, scatter_dimension=0, tiled=True).astype(f32)
    in_norm, g_gain1, g_bias1 = norm_back(n1, inv1, vecs[0], grad_norm1)
    grad_inputs = grad_middle + in_norm

    def owned_rows(g):
        return lax.psum_scatter(g, "fsdp", scatter_dimension=0, tiled=True)

    def owned_cols(g, groups):
        g = lax.psum_scatter(g.reshape(dpn, width // dpn, -1), "fsdp", scatter_dimension=1, tiled=True)
        g = lax.all_to_all(g, tp, 0, 0, tiled=True)
        g = g.reshape(dpn, rows, groups, -1).transpose(1, 2, 0, 3)
        return g.reshape(rows, -1).astype(f32)

    o_down = owned_rows(g_down).astype(f32)
    o_up = owned_cols(g_up, 1)
    o_out = owned_rows(g_out).astype(f32)
    o_qkv = owned_cols(g_qkv, 3)
    small = jnp.stack([g_gain1, g_bias1, g_gain2, g_bias2]).reshape(4, dpn * fsn, rows).transpose(1, 0, 2)
    small = lax.psum_scatter(small.reshape(dpn * fsn, 4 * rows), ("dp", "fsdp"), scatter_dimension=0, tiled=True).reshape(4, rows)
    return (result[None], grad_inputs[None], o_qkv, o_out, o_up, o_down, small[0], small[1], small[2], small[3])


CHUNKS = 2
SENDS = 320
ARRIVALS = 320
MESH = pl.DeviceIdType.MESH


def layer_kernel(
    phon_len, acou_len, row_item, frames, cot, vec_in, wq_in, wo_in, wu_in, wd_in,
    o_res, o_in, o_q, o_o, o_u, o_d, o_small,
    VG, VEC, WQ, WO, WU, WD, N1F, INV1, N1, COT, QKV, ATT, LSE, PA, PB,
    LA1, LA2, LB1, LB2, LC1, LC2, LD1, LD2,
    MID, N2F, INV2, NORM2, ACT, SLOPE, GUP, GPROJ,
    GD, GU, GO, GQ, YD, YU, YO, YQ, SU, SQ, ZD, ZU, ZO, ZQ, RU, RQ,
    SM, SM1, SM2, SM3, SM4, SM5,
    ssem, rsem,
):
    dpn, fsn = lax.axis_size("dp"), lax.axis_size("fsdp")
    lens = (phon_len[row_item[0]], acou_len[row_item[0]])
    nz = fsn // 2
    width = frames.shape[1]
    own = frames.shape[0]
    part = width // dpn
    rows = wu_in.shape[0]
    d, f = lax.axis_index("dp"), lax.axis_index("fsdp")
    c, x = lax.rem(d, 2), lax.div(d, 2)
    y, z = lax.rem(f, 2), lax.div(f, 2)
    core = d + 1 - 2 * c
    far = lax.rem(d + 2, dpn)
    other = lax.rem(core + 2, dpn)
    order = (d, core, far, other)
    pair = (d, f + 1 - 2 * y)
    count = {"send": 0, "arrive": 0}
    sent = []

    def slots(n):
        base = count["arrive"]
        count["arrive"] += n
        assert count["arrive"] <= ARRIVALS
        return base

    def push(src, dst, slot, device, when=None):
        i = count["send"]
        count["send"] += 1
        assert i < SENDS
        copy = pltpu.make_async_remote_copy(src, dst, ssem.at[i], rsem.at[slot], device_id=device, device_id_type=MESH)
        if when is None:
            copy.start()
        else:
            pl.when(when)(lambda: copy.start())
        sent.append((when, copy))

    def push_each(n, piece, compute):
        first = count["send"]
        count["send"] += n

        def copy_of(i):
            src, dst, slot, device = piece(i)
            return pltpu.make_async_remote_copy(src, dst, ssem.at[first + i], rsem.at[slot], device_id=device, device_id_type=MESH)

        def step(i, carry):
            compute(i)
            copy_of(i).start()
            return carry

        lax.fori_loop(0, n, step, 0)
        sent.extend((None, copy_of(i)) for i in range(n))

    def sent_out(copies):
        for when, copy in copies:
            if when is None:
                copy.wait_send()
            else:
                pl.when(when)(lambda copy=copy: copy.wait_send())

    def arrive(ref, slot):
        pltpu.make_async_remote_copy(ref, ref, ssem.at[0], rsem.at[slot], device_id=pair, device_id_type=MESH).wait_recv()

    def zpeer(k):
        return lax.rem(z + k, nz)

    barrier = pltpu.get_barrier_semaphore()
    peers = [(lax.rem(d + k, dpn), f) for k in range(1, dpn)] + [(d, lax.rem(f + k, fsn)) for k in range(1, fsn)]
    for device in peers:
        pl.semaphore_signal(barrier, inc=1, device_id=device, device_id_type=MESH)
    pl.semaphore_wait(barrier, len(peers))

    def tile(i):
        return slice(i * part, (i + 1) * part)

    vec_f, vec_d = slots(fsn), slots(dpn)
    for k in range(1, fsn):
        push(vec_in, VG.at[d, f], vec_f + f, (d, lax.rem(f + k, fsn)))
    mix_q, mix_u = slots(dpn * 3), slots(dpn)

    def q_cols(dd, j):
        return pl.ds(pl.multiple_of(j * width + dd * part, part), part)

    def u_cols(dd):
        return pl.ds(pl.multiple_of(dd * width, width), width)

    for k in range(1, dpn):
        dd = lax.rem(d + k, dpn)
        for j in range(3):
            push(wq_in.at[:, q_cols(dd, j)], WQ.at[d, f, :, tile(j)], mix_q + d * 3 + j, (dd, f))
    for k in range(1, dpn):
        dd = lax.rem(d + k, dpn)
        push(wu_in.at[:, u_cols(dd)], WU.at[d, f], mix_u + d, (dd, f))
    zq, zo, zu, zd = slots(nz), slots(nz), slots(nz), slots(nz)
    yq, yo, yu, yd = slots(nz), slots(nz), slots(nz), slots(nz)
    def clip(v):
        return jnp.clip(v, 0, nz - 1)

    def along(ref_at, zs):
        for side in (1, -1):
            to = z + side
            push(ref_at(f), ref_at(f), zs + z, (d, clip(to) * 2 + y), when=(to >= 0) & (to < nz))

    def across_own(ref_at, ys):
        push(ref_at(f), ref_at(f), ys + z, pair)

    def hop(ref_at, zs, ys, h):
        for side in (1, -1):
            src, to = z + side * h, z - side
            here = (src >= 0) & (src < nz)
            ref, src = ref_at(clip(src) * 2 + y), clip(src)
            pl.when(here)(lambda: arrive(ref, zs + src))
            push(ref, ref, zs + src, (d, clip(to) * 2 + y), when=here & (to >= 0) & (to < nz))
            push(ref, ref, ys + src, pair, when=here)

    def forward(ref_at, zs, ys, first=1, last=None):
        for h in range(first, nz if last is None else last + 1):
            hop(ref_at, zs, ys, h)

    def gathered(ref_at, ys):
        for zz in range(nz):
            arrive(ref_at(2 * zz + 1 - y), ys + zz)

    def q_at(s):
        return WQ.at[:, s]

    def o_at(s):
        return WO.at[s]

    def u_at(s):
        return WU.at[:, s]

    def d_at(s):
        return WD.at[s]

    WO[f] = wo_in[...]
    WD[f] = wd_in[...]
    along(o_at, zo)
    across_own(o_at, yo)
    across_own(d_at, yd)
    VG[d, f] = vec_in[...]
    for j in range(3):
        WQ[d, f, :, tile(j)] = wq_in[:, q_cols(d, j)]
    WU[d, f] = wu_in[:, u_cols(d)]

    def norm_rows(v, nf, inv):
        n, i = norm_parts(v)
        nf[...] = n
        inv[...] = i

    norm_rows(frames[...].astype(f32), N1F, INV1)
    for k in range(1, fsn):
        s = lax.rem(f + k, fsn)
        arrive(VG.at[d, s], vec_f + s)
    for k in range(1, dpn):
        push(VG.at[d], VG.at[d], vec_d + d, (lax.rem(d + k, dpn), f))

    for k in range(1, dpn):
        s = lax.rem(d + k, dpn)
        for j in range(3):
            arrive(WQ.at[s, f, :, tile(j)], mix_q + s * 3 + j)
    along(q_at, zq)
    across_own(q_at, yq)
    for k in range(1, dpn):
        s = lax.rem(d + k, dpn)
        arrive(VG.at[s], vec_d + s)
    group = 128 // rows
    for m in range(width // 128):
        total = VG[(m * group) // fsn, (m * group) % fsn]
        for j in range(1, group):
            total = total + VG[(m * group + j) // fsn, (m * group + j) % fsn]
        VEC[:, m * 128 : (m + 1) * 128] = total

    step = own // CHUNKS

    def ag_start(ref, base):
        for device in (far, core):
            for h in range(CHUNKS):
                piece = ref.at[d, h * step : (h + 1) * step]
                push(piece, piece, base + d * CHUNKS + h, (device, f))

    def ag_forward(ref, base):
        for h in range(CHUNKS):
            piece = ref.at[far, h * step : (h + 1) * step]
            arrive(piece, base + far * CHUNKS + h)
            push(piece, piece, base + far * CHUNKS + h, (core, f))

    def ag_wait(ref, base, b):
        for h in range(CHUNKS):
            arrive(ref.at[b, h * step : (h + 1) * step], base + b * CHUNKS + h)

    def rs_near(P, L1, base, compute, between=lambda: None):
        for j, hi in enumerate((1 - x, x)):
            b_send, b_keep = hi * 2 + 1 - c, hi * 2 + c
            compute(b_send)
            push(P.at[b_send], L1.at[j], base + j, (core, f))
            compute(b_keep)
            if j == 0:
                between()

    def rs_far(P, L1, L2, base):
        b_far = (1 - x) * 2 + c
        arrive(L1.at[0], base)
        P[b_far] = (P[b_far].astype(f32) + L1[0].astype(f32)).astype(bf16)
        push(P.at[b_far], L2, base + 2, (far, f))

    def rs_send(P, L1, L2, base, compute):
        rs_near(P, L1, base, compute, lambda: rs_far(P, L1, L2, base))

    def rs_total(P, L1, L2, base):
        arrive(L1.at[1], base + 1)
        arrive(L2, base + 2)
        return P[d].astype(f32) + L1[1].astype(f32) + L2[...].astype(f32)

    def lines(b):
        return pl.ds(pl.multiple_of(b * own, own), own)

    ag1, agc, ag2, agp = slots(dpn * CHUNKS), slots(dpn * CHUNKS), slots(dpn * CHUNKS), slots(dpn * CHUNKS)
    rs1, rs2, rs3, rs4 = slots(3), slots(3), slots(3), slots(3)

    N1[d] = (N1F[...] * VEC[0:1, :] + VEC[1:2, :]).astype(bf16)
    COT[d] = cot[...]
    ag_start(N1, ag1)
    forward(q_at, zq, yq, 1, 1)
    forward(o_at, zo, yo, 1, 1)
    forward(q_at, zq, yq, 2, 2)
    forward(o_at, zo, yo, 2, 2)
    for k in range(1, dpn):
        s = lax.rem(d + k, dpn)
        arrive(WU.at[s, f], mix_u + s)
    along(u_at, zu)
    forward(q_at, zq, yq, 3)
    forward(o_at, zo, yo, 3)
    across_own(u_at, yu)
    ag_forward(N1, ag1)
    ag_start(COT, agc)
    forward(u_at, zu, yu, 1, 1)
    along(d_at, zd)
    gathered(q_at, yq)
    for n, b in enumerate(order):
        if n in (1, 3):
            ag_wait(N1, ag1, b)
        QKV[lines(b), :] = dot(N1[b], WQ[...].reshape(width, 3 * part), 1, 0).astype(bf16)
    attn_fwd_kernel(lens, QKV, ATT, LSE)
    ag_forward(COT, agc)
    gathered(o_at, yo)

    def proj(b):
        PA[b] = dot(ATT[lines(b), :], WO[...].reshape(part, width), 1, 0).astype(bf16)

    proj_sends = len(sent)
    rs_send(PA, LA1, LA2, rs1, proj)
    proj_sends = sent[proj_sends:]
    forward(u_at, zu, yu, 2)
    forward(d_at, zd, yd, 1, 1)
    MID[...] = frames[...].astype(f32) + rs_total(PA, LA1, LA2, rs1)
    norm_rows(MID[...], N2F, INV2)
    NORM2[d] = (N2F[...] * VEC[2:3, :] + VEC[3:4, :]).astype(bf16)
    ag_start(NORM2, ag2)
    gathered(u_at, yu)

    def wide(i):
        return pl.ds(pl.multiple_of(i * 2 * part, part), 2 * part)

    def halves(step):
        lax.fori_loop(0, dpn // 2, lambda i, carry: (step(i), carry)[1], 0)

    def up(b):
        def half(i):
            u = dot(NORM2[b], WU[:, :, :, wide(i)].reshape(width, 2 * part), 1, 0)
            cdf = 0.5 * (1.0 + lax.erf(u * (0.5**0.5)))
            ACT[b, :, wide(i)] = (u * cdf).astype(bf16)
            SLOPE[b, :, wide(i)] = cdf + u * (jnp.exp(-0.5 * u * u) * (1.0 / (2.0 * jnp.pi) ** 0.5))

        halves(half)

    up(d)
    forward(d_at, zd, yd, 2, 2)
    ag_wait(NORM2, ag2, core)
    up(core)
    forward(d_at, zd, yd, 3)
    ag_forward(NORM2, ag2)
    up(far)
    ag_wait(NORM2, ag2, other)
    up(other)
    ag_wait(COT, agc, core)
    ag_wait(COT, agc, other)
    y_d, y_u, y_o, y_q = slots(nz), slots(dpn), slots(1), slots(dpn)
    z_d, z_u, z_o, z_q = slots(nz), slots(nz * dpn), slots(nz), slots(nz * dpn)
    big = wd_in.shape[0]

    def against(a, b, i):
        return dot(a[:, :, pl.ds(pl.multiple_of(i * part, part), part)].reshape(dpn * own, part), b, 0, 0).astype(bf16)

    def grad_down(k):
        GD[zpeer(k + 1)] = against(ACT, COT[...].reshape(dpn * own, width), zpeer(k + 1)).reshape(2, big, width)

    push_each(nz, lambda k: (GD.at[zpeer(k + 1), 1 - y], YD.at[zpeer(k + 1)], y_d + zpeer(k + 1), pair), grad_down)
    gathered(d_at, yd)
    per = fsn // dpn

    def grad_hidden(b):
        for i in range(dpn):
            g = dot(COT[b], WD[i * per : (i + 1) * per].reshape(part, width), 1, 1)
            GUP[b, :, tile(i)] = (g * SLOPE[b, :, tile(i)]).astype(bf16)
        for i in range(dpn):
            PB[b, :, tile(i)] = dot(GUP[b], WU[i].reshape(part, width), 1, 1).astype(bf16)

    norm2_sends = len(sent)
    rs_send(PB, LB1, LB2, rs2, grad_hidden)
    norm2_sends = sent[norm2_sends:]

    def add(a, b):
        return (a.astype(f32) + b.astype(f32)).astype(bf16)

    def sum_d(k):
        j = zpeer(k)
        arrive(YD.at[j], y_d + j)
        YD[j] = add(GD[j, y], YD[j])
        if k < nz:
            push(YD.at[j], ZD.at[z], z_d + z, (d, j * 2 + y))

    def sum_chunk(G, Y, S, Z, ys, zs, i):
        arrive(Y.at[i], ys + i)
        S[:, i] = add(G[i, :, y], Y[i])
        for k in range(1, nz):
            zz = zpeer(k)
            push(S.at[zz, i], Z.at[z, i], zs + z * dpn + i, (d, zz * 2 + y))

    def sum_u(i):
        sum_chunk(GU, YU, SU, ZU, y_u, z_u, i)

    def sum_q(i):
        sum_chunk(GQ, YQ, SQ, ZQ, y_q, z_q, i)

    sum_d(1)
    sent_out(proj_sends)

    def down(b):
        def half(i):
            PA[b, :, wide(i)] = dot(ACT[b], WD[:, :, wide(i)].reshape(width, 2 * part), 1, 0).astype(bf16)

        halves(half)

    rs_near(PA, LC1, rs3, down)
    sum_d(2)
    MIDG = N2F
    grad2 = rs_total(PB, LB1, LB2, rs2)
    mid_norm, gain2, bias2 = norm_back(N2F[...], INV2[...], VEC[2:3, :], grad2)
    MIDG[...] = cot[...].astype(f32) + mid_norm
    GPROJ[d] = MIDG[...].astype(bf16)
    ag_start(GPROJ, agp)
    sum_d(3)

    def grad_up(i):
        GU[i] = against(NORM2, GUP[...].reshape(dpn * own, width), i).reshape(nz, 2, rows, width)

    push_each(dpn, lambda i: (GU.at[i, :, 1 - y], YU.at[i], y_u + i, pair), grad_up)

    GATT, GQKV = GUP.at[:, :, :part], ACT.at[:, :, : 3 * part]
    DK, DV = SLOPE.at[:, :, :part], SLOPE.at[:, :, part : 2 * part]

    def grad_heads(b):
        GATT[b] = dot(GPROJ[b], WO[...].reshape(part, width), 1, 1).astype(bf16)

    grad_heads(d)
    ag_forward(GPROJ, agp)
    rs_far(PA, LC1, LC2, rs3)
    grad_heads(far)
    ag_wait(GPROJ, agp, core)
    grad_heads(core)
    ag_wait(GPROJ, agp, other)
    grad_heads(other)

    g = dot(ATT[...], GPROJ[...].reshape(dpn * own, width), 0, 0).astype(bf16)
    GO[...] = g.reshape(nz, 2, rows, width)
    push(GO.at[:, 1 - y], YO, y_o, pair)
    sum_d(nz)
    sum_u(0)

    attn_bwd_kernel(lens, QKV, GATT, LSE, GQKV, DK, DV, {2: lambda: sum_u(1), 1: lambda: sum_u(2), 0: lambda: sum_u(3)})

    def grad_q(i):
        GQ[i] = against(N1, GQKV[...].reshape(dpn * own, 3 * part), i).reshape(nz, 2, rows, 3 * part)

    push_each(dpn, lambda i: (GQ.at[i, :, 1 - y], YQ.at[i], y_q + i, pair), grad_q)

    sent_out(norm2_sends)

    def grad_first(b):
        def half(i):
            PB[b, :, wide(i)] = dot(GQKV[b], WQ[pl.ds(2 * i, 2)].reshape(2 * part, 3 * part), 1, 1).astype(bf16)

        halves(half)

    rs_send(PB, LD1, LD2, rs4, grad_first)

    arrive(YO, y_o)
    YO[...] = add(GO[:, y], YO[...])
    for k in range(1, nz):
        zz = zpeer(k)
        push(YO.at[zz], ZO.at[z], z_o + z, (d, zz * 2 + y))
    for i in range(dpn // 2):
        sum_q(i)
    grad1 = rs_total(PB, LD1, LD2, rs4)
    in_norm, gain1, bias1 = norm_back(N1F[...], INV1[...], VEC[0:1, :], grad1)
    o_in[...] = MIDG[...] + in_norm
    small = jnp.concatenate([v.reshape(1, width) for v in (gain1, bias1, gain2, bias2)] + [jnp.zeros((4, width), f32)], axis=0)
    for i in range(dpn):
        SM[i] = small[:, tile(i)]
    sm_d, sm_y, sm_z = slots(dpn), slots(1), slots(nz)
    for k in range(1, dpn):
        dd = lax.rem(d + k, dpn)
        push(SM.at[dd], SM1.at[d], sm_d + d, (dd, f))

    for i in range(dpn // 2, dpn):
        sum_q(i)
    SD, SO = YD, YO

    def settle(S, Z, zs, pieces=1):
        total = S[z].astype(f32)
        for k in range(1, nz):
            zz = zpeer(k)
            for i in range(pieces):
                arrive(Z.at[zz, i] if pieces > 1 else Z.at[zz], zs + zz * pieces + i)
            total = total + Z[zz].astype(f32)
        return total

    TU, TQ = GUP.at[:, :rows], GUP.at[:, rows : 2 * rows, : 3 * part]
    back_u, back_q = slots(dpn), slots(dpn)
    TU[...] = settle(SU, ZU, z_u, dpn).astype(bf16)
    for k in range(1, dpn):
        dd = lax.rem(d + k, dpn)
        push(TU.at[dd], RU.at[d], back_u + d, (dd, f))
    RU[d] = TU[d]

    o_d[...] = settle(SD, ZD, z_d)
    o_o[...] = settle(SO, ZO, z_o)

    total = SM[d]
    for k in range(1, dpn):
        s = lax.rem(d + k, dpn)
        arrive(SM1.at[s], sm_d + s)
        total = total + SM1[s]
    SM2[...] = total
    push(SM2, SM3, sm_y, pair)

    arrive(SM3, sm_y)
    SM4[...] = SM2[...] + SM3[...]
    for k in range(1, nz):
        push(SM4, SM5.at[z], sm_z + z, (d, zpeer(k) * 2 + y))

    TQ[...] = settle(SQ, ZQ, z_q, dpn).astype(bf16)
    for k in range(1, dpn):
        dd = lax.rem(d + k, dpn)
        push(TQ.at[dd], RQ.at[d], back_q + d, (dd, f))
    RQ[d] = TQ[d]

    o_res[...] = (MID[...] + rs_total(PA, LC1, LC2, rs3)).astype(bf16)
    for k in range(1, dpn):
        s = lax.rem(d + k, dpn)
        arrive(RU.at[s], back_u + s)
    for s in range(dpn):
        o_u[:, s * width : (s + 1) * width] = RU[s].astype(f32)
    for k in range(1, dpn):
        s = lax.rem(d + k, dpn)
        arrive(RQ.at[s], back_q + s)
    for s in range(dpn):
        for j in range(3):
            o_q[:, j * width + s * part : j * width + (s + 1) * part] = RQ[s, :, tile(j)].astype(f32)
    total = SM4[...]
    for k in range(1, nz):
        zz = zpeer(k)
        arrive(SM5.at[zz], sm_z + zz)
        total = total + SM5[zz]
    o_small[...] = total

    waited = set(id(copy) for _, copy in proj_sends + norm2_sends)
    sent_out([(when, copy) for when, copy in sent if id(copy) not in waited])


def in_one_kernel(frames, cotangent, phon_len, acou_len, row_item, w_qkv, w_out, w_up, w_down, ln1_gain, ln1_bias, ln2_gain, ln2_bias):
    dpn, fsn = lax.axis_size("dp"), lax.axis_size("fsdp")
    nz = fsn // 2
    own, width = frames.shape[1:]
    length = dpn * own
    part = width // dpn
    rows = w_up.shape[0]
    big = w_down.shape[0]
    place = lax.axis_index("fsdp") * rows % 128
    vec = jnp.stack([ln1_gain, ln1_bias, ln2_gain, ln2_bias]).astype(f32)
    vec = jnp.pad(vec, ((0, 4), (0, 128 - rows)))
    vec = jnp.roll(vec, place, axis=1)

    def buf(*shape, dtype=bf16):
        return pltpu.VMEM(shape, dtype)

    full = buf(dpn, own, width)
    land = [buf(2, own, width), buf(own, width)]
    scratch = [
        buf(dpn, fsn, 8, 128, dtype=f32), buf(8, width, dtype=f32),
        buf(dpn, fsn, rows, 3 * part), buf(fsn, rows, width), buf(dpn, fsn, rows, width), buf(fsn, big, width),
        buf(own, width, dtype=f32), buf(own, 1, dtype=f32), full, full,
        buf(length, 3 * part), buf(length, part), buf(8, length, dtype=f32), full, full,
        *land, *land, *land, *land,
        buf(own, width, dtype=f32), buf(own, width, dtype=f32), buf(own, 1, dtype=f32),
        full, full, buf(dpn, own, width, dtype=f32), full, full,
        buf(nz, 2, big, width), buf(dpn, nz, 2, rows, width), buf(nz, 2, rows, width), buf(dpn, nz, 2, rows, 3 * part),
        buf(nz, big, width), buf(dpn, nz, rows, width), buf(nz, rows, width), buf(dpn, nz, rows, 3 * part),
        buf(nz, dpn, rows, width), buf(nz, dpn, rows, 3 * part),
        buf(nz, big, width), buf(nz, dpn, rows, width), buf(nz, rows, width), buf(nz, dpn, rows, 3 * part),
        buf(dpn, rows, width), buf(dpn, rows, 3 * part),
        buf(dpn, 8, part, dtype=f32), buf(dpn, 8, part, dtype=f32), buf(8, part, dtype=f32), buf(8, part, dtype=f32),
        buf(8, part, dtype=f32), buf(nz, 8, part, dtype=f32),
        pltpu.SemaphoreType.DMA((SENDS,)), pltpu.SemaphoreType.DMA((ARRIVALS,)),
    ]
    outs = pl.pallas_call(
        layer_kernel,
        out_shape=(
            jax.ShapeDtypeStruct((own, width), bf16),
            jax.ShapeDtypeStruct((own, width), f32),
            jax.ShapeDtypeStruct((rows, 3 * width), f32),
            jax.ShapeDtypeStruct((rows, width), f32),
            jax.ShapeDtypeStruct((rows, dpn * width), f32),
            jax.ShapeDtypeStruct((big, width), f32),
            jax.ShapeDtypeStruct((8, part), f32),
        ),
        in_specs=[SMEM] * 3 + [VMEM] * 7,
        out_specs=(VMEM,) * 7,
        scratch_shapes=scratch,
        compiler_params=pltpu.CompilerParams(collective_id=0, has_side_effects=True, vmem_limit_bytes=67043328),
        name="layer",
    )(phon_len, acou_len, row_item, frames[0], cotangent[0], vec, w_qkv, w_out, w_up, w_down)
    small = lax.dynamic_slice(outs[6], (0, lax.axis_index("fsdp") * rows), (4, rows))
    return (outs[0][None], outs[1][None], *outs[2:6], small[0], small[1], small[2], small[3])


def on_device(*args):
    dpn, fsn, rows, width = lax.axis_size("dp"), lax.axis_size("fsdp"), args[7].shape[0], args[0].shape[2]
    fits = dpn == 4 and args[0].shape[1] == BLOCK and fsn % dpn == 0 and rows % 16 == 0 and 128 % rows == 0 and width == 2 * dpn * args[8].shape[0]
    return (in_one_kernel if fits else with_collectives)(*args)


def solution(mesh):
    split = P(("dp", "fsdp"), None)
    vec = P(("dp", "fsdp"))
    acts = P("fsdp", "dp", None)
    return jax.shard_map(
        on_device,
        mesh=mesh,
        in_specs=(acts, acts, P(), P(), P("fsdp"), split, split, split, split, vec, vec, vec, vec),
        out_specs=(acts, acts, split, split, split, split, vec, vec, vec, vec),
        check_vma=False,
    )
```

profile of v0, /device:TPU:0, one launch (start us, length us, event | category | flops | bytes accessed | tf_op | source)
XLA Modules:
  0.0 177.7 jit_solution(17850813233122566991)
XLA Ops:
  1.3 0.0 copy-start.8
  1.3 0.0 copy-start.5
  1.3 0.0 copy-start.6
  1.4 0.0 copy-start.7
  1.4 0.6 copy-done.8
  2.0 0.0 copy-done.5
  2.0 0.0 copy-done.6
  2.0 0.0 copy-done.7
  2.0 0.7 fusion.6.vec_in
  2.7 166.8 %layer.1 = (bf16[256,1024]{1,0:T(8,128)(2,1)}, f32[256,1024]{1,0:T(8,128)}, f32[32,3072]{1,0:T(8,128)}, f32[32,1024]{1,0:T(8,128)}, f32[32,4096]{1,0:T(8,128)}, /*index=5*/f32[128,1024]{1,0:T(8,128)}, f32[8,256]{1,0:T(8,128)}) custom-call(s32[8]{0:T(128)} %phon_len.1, s32[8]{0:T(128)} %acou_len.1, s32[1]{0:T(128)S(6)} %copy.29.row_item, ...), custom_call_target="tpu_custom_call" | custom-call | tf_op jit(solution)/shard_map/layer/pallas_call | solution.py:761
  169.5 0.0 copy-start
  169.5 0.8 constant_dynamic-slice_fusion
  170.4 0.5 slice_bitcast_fusion
  170.9 1.9 %copy.30 = bf16[1,256,1024]{2,1,0:T(8,128)(2,1)} copy(bf16[1,256,1024]{2,1,0:T(8,128)(2,1)} %bitcast.17) | data formatting | bytes 1048576
  172.8 0.0 copy-done
  172.8 0.0 copy-start.3
  172.8 1.0 copy.31
  173.8 0.3 copy-done.3
  174.0 0.0 copy-start.4
  174.0 0.0 copy-start.2
  174.0 0.7 copy.32
  174.8 0.2 copy-done.4
  175.0 0.7 copy.33
  175.7 0.0 copy-done.2
  175.7 0.0 copy-start.1
  175.7 0.8 copy.34
  176.5 0.4 copy-done.1
  176.9 0.8 copy.35
  (1 shorter events, 0.0 us)
Async XLA Ops:
  1.3 0.7 copy-start.8
  1.3 0.7 copy-start.5
  1.3 0.7 copy-start.6
  1.4 0.7 copy-start.7
  169.5 3.3 %copy-start = (f32[256,1024]{1,0:T(8,128)S(1)}, f32[256,1024]{1,0:T(8,128)}, u32[]{:S(2)}) copy-start(f32[256,1024]{1,0:T(8,128)} %get-tuple-element.18) | copy-start | bytes 3145732
  172.8 1.2 copy-start.3
  174.0 1.0 copy-start.4
  174.0 1.7 copy-start.2
  175.7 1.2 copy-start.1
where the time goes:
time: 178 us
  Pallas kernels  167 us (94%)
  local copies, waits for them, and re-layouts  8.83 us (5%)
    pallas_call x1, Pallas kernels, in_one_kernel(): pl.pallas_call(layer_kernel, out_shape=(jax.ShapeDtypeStruct((own, width)...  167 us
    unnamed x24, local copies, waits for them, and re-layouts  7.45 us

commit v1 on v0

--- a/solution.py
+++ b/solution.py
@@ -721,6 +721,32 @@
 
     waited = set(id(copy) for _, copy in proj_sends + norm2_sends)
     sent_out([(when, copy) for when, copy in sent if id(copy) not in waited])
+
+
+def copy_kernel(*refs):
+    n = (len(refs) - 1) // 3
+    ins, outs, held, sem = refs[:n], refs[n : 2 * n], refs[2 * n : 3 * n], refs[3 * n]
+    first = [pltpu.make_async_copy(a, h, sem.at[0, i]) for i, (a, h) in enumerate(zip(ins, held))]
+    second = [pltpu.make_async_copy(h, o, sem.at[1, i]) for i, (h, o) in enumerate(zip(held, outs))]
+    for copy in first:
+        copy.start()
+    for one, two in zip(first, second):
+        one.wait()
+        two.start()
+    for copy in second:
+        copy.wait()
+
+
+def copied(arrays):
+    anywhere = pl.BlockSpec(memory_space=pl.ANY)
+    return pl.pallas_call(
+        copy_kernel,
+        out_shape=tuple(jax.ShapeDtypeStruct(a.shape, a.dtype) for a in arrays),
+        in_specs=[anywhere] * len(arrays),
+        out_specs=(anywhere,) * len(arrays),
+        scratch_shapes=[pltpu.VMEM(a.shape, a.dtype) for a in arrays] + [pltpu.SemaphoreType.DMA((2, len(arrays)))],
+        name="results",
+    )(*arrays)
 
 
 def in_one_kernel(frames, cotangent, phon_len, acou_len, row_item, w_qkv, w_out, w_up, w_down, ln1_gain, ln1_bias, ln2_gain, ln2_bias):
@@ -776,6 +802,7 @@
         name="layer",
     )(phon_len, acou_len, row_item, frames[0], cotangent[0], vec, w_qkv, w_out, w_up, w_down)
     small = lax.dynamic_slice(outs[6], (0, lax.axis_index("fsdp") * rows), (4, rows))
+    outs = copied(outs[:6])
     return (outs[0][None], outs[1][None], *outs[2:6], small[0], small[1], small[2], small[3])
 
 

time: 178 us -> 174 us (0.978)
  local copies, waits for them, and re-layouts: 8.83 us -> 1.95 us
  Pallas kernels: 167 us -> 170 us
    unnamed x24 -> x8, local copies, waits for them, and re-layouts: 7.45 us -> 0.67 us
    pallas_call x0 -> x1, Pallas kernels: none -> 2.98 us  [copied(): pl.pallas_call(copy_kernel, out_shape=tuple((jax.ShapeDtypeStruct(a.shape...]
where the time goes in v1:
time: 174 us
  Pallas kernels  170 us (98%)
  local copies, waits for them, and re-layouts  1.95 us (1%)
    pallas_call x1, Pallas kernels, in_one_kernel(): pl.pallas_call(layer_kernel, out_shape=(jax.ShapeDtypeStruct((own, width)...  167 us

profile of v1, /device:TPU:0, one launch (start us, length us, event | category | flops | bytes accessed | tf_op | source)
XLA Modules:
  0.0 173.8 jit_solution(18138427845677108943)
XLA Ops:
  1.3 0.0 copy-start.3
  1.3 0.0 copy-start
  1.3 0.0 copy-start.1
  1.4 0.0 copy-start.2
  1.4 0.6 copy-done.3
  2.0 0.0 copy-done
  2.0 0.0 copy-done.1
  2.0 0.0 copy-done.2
  2.0 0.7 fusion.6.vec_in
  2.7 166.8 %layer.1 = (bf16[256,1024]{1,0:T(8,128)(2,1)}, f32[256,1024]{1,0:T(8,128)}, f32[32,3072]{1,0:T(8,128)}, f32[32,1024]{1,0:T(8,128)}, f32[32,4096]{1,0:T(8,128)}, /*index=5*/f32[128,1024]{1,0:T(8,128)}, f32[8,256]{1,0:T(8,128)}) custom-call(s32[8]{0:T(128)} %phon_len.1, s32[8]{0:T(128)} %acou_len.1, s32[1]{0:T(128)S(6)} %copy.23.row_item, ...), custom_call_target="tpu_custom_call" | custom-call | tf_op jit(solution)/shard_map/layer/pallas_call | solution.py:787
  169.6 3.0 %results.1 = (bf16[256,1024]{1,0:T(8,128)(2,1)}, f32[256,1024]{1,0:T(8,128)}, f32[32,3072]{1,0:T(8,128)}, f32[32,1024]{1,0:T(8,128)}, f32[32,4096]{1,0:T(8,128)}, /*index=5*/f32[128,1024]{1,0:T(8,128)}) custom-call(bf16[256,1024]{1,0:T(8,128)(2,1)} %get-tuple-element.23.refs_0_, f32[256,1024]{1,0:T(8,128)} %get-tuple-element.24.refs_1_, ...), custom_call_target="tpu_custom_call" | custom-call | tf_op jit(solution)/shard_map/results/pallas_call | solution.py:742
  172.5 0.8 constant_dynamic-slice_fusion
  173.3 0.5 slice_bitcast_fusion
  (1 shorter events, 0.0 us)
Async XLA Ops:
  1.3 0.7 copy-start.3
  1.3 0.7 copy-start
  1.3 0.7 copy-start.1
  1.4 0.7 copy-start.2
